TPU v7x, 512 devices: a whole 4x4x16 slice. The times are simulated.
512 devices in a mesh: crop: 8 (over z_lo, core), axial: 64 (over x, y, z_hi).
Axes of the slice: x: 4, y: 4, z: 16 (z_hi: 4, z_lo: 4; z = z_hi * 4 + z_lo), core: 2. Of those that a mesh axis runs over, the one named last changes fastest.
Arguments:
- pair: bfloat16 [8, 256, 256, 128], P('crop', 'axial'), may hold values from -6 to 6
- crop_mask: int32 [8, 256], P('crop'), may hold values 0 or 1
- weights: bfloat16 [128, 768], replicated, may hold values from -0.5 to 0.5
- probe_signs: int32 [128, 768], replicated, may hold values from 0 to 1
Outputs:
- pair_out: bfloat16 [8, 256, 256, 128], P('crop', 'axial')
- curvature: float32 [128, 768], replicated
All inputs are finite; a program needn't handle non-finite values. No bound on the sum of `crop_mask` on one device may be relied on, other than what follows from the above.
Results may differ from a plain program's by a relative error of at most 0.006.
Values may be sent and summed in bfloat16 or wider, within the bound.
A program may use at most 64 MiB of HBM per device.

v0:
```python
import jax
import jax.numpy as jnp
from jax import lax
from jax.sharding import PartitionSpec as P


def norm_axis(value, axis):
    mean = jnp.mean(value, axis=axis, keepdims=True)
    centered = value - mean
    var = jnp.mean(centered * centered, axis=axis, keepdims=True)
    return centered * lax.rsqrt(var + 1e-05)


def project_in(w_in, zn_bf, mask_pair):
    proj = jnp.einsum(
        "rnc,cd->drn", zn_bf, w_in.astype(jnp.bfloat16), preferred_element_type=jnp.float32
    )
    hid = proj.shape[0] // 4
    a_full = jax.nn.sigmoid(proj[hid : 2 * hid]) * proj[:hid] * mask_pair
    b_full = jax.nn.sigmoid(proj[3 * hid :]) * proj[2 * hid : 3 * hid] * mask_pair
    return (a_full, b_full)


def head(w_head, x_full, zn_bf):
    chans = zn_bf.shape[2]
    w_gate = w_head[:, :chans].astype(jnp.bfloat16)
    w_out = w_head[:, chans:].astype(jnp.bfloat16)
    x_norm = norm_axis(x_full, 0).astype(jnp.bfloat16)
    out_proj = jnp.einsum("hrn,hc->rnc", x_norm, w_out, preferred_element_type=jnp.float32)
    gating = jax.nn.sigmoid(
        jnp.einsum("rnc,cd->rnd", zn_bf, w_gate, preferred_element_type=jnp.float32)
    )
    return gating * out_proj


def tri_out(left, right):
    return jnp.einsum("cik,cjk->cij", left, right, preferred_element_type=jnp.float32)


def slab_products(slabs):
    a_ch, b_ch, ta_ch, tb_ch = slabs
    x_ch = tri_out(a_ch, b_ch).astype(jnp.bfloat16)
    tx_ch = (tri_out(ta_ch, b_ch) + tri_out(a_ch, tb_ch)).astype(jnp.bfloat16)
    return (x_ch, tx_ch, a_ch, b_ch)


def shards(pair, crop_mask, weights, probe_signs):
    pair_rows = pair[0]
    rows = pair_rows.shape[0]
    width = pair_rows.shape[1]
    chans = weights.shape[0]
    h4 = weights.shape[1] - 2 * chans
    mask = crop_mask[0].astype(jnp.float32)
    start = lax.axis_index("axial") * rows
    mask_rows = lax.dynamic_slice_in_dim(mask, start, rows, 0)
    mask_pair = mask_rows[:, None] * mask[None, :]
    zn = norm_axis(pair_rows.astype(jnp.float32), 2).astype(jnp.bfloat16)
    w_all = weights.astype(jnp.float32)
    probe = (2 * probe_signs - 1).astype(jnp.float32) * (1.0 / jnp.sqrt(jnp.float32(chans)))
    w_in, w_head = (w_all[:, :h4], w_all[:, h4:])
    v_in, v_head = (probe[:, :h4], probe[:, h4:])
    fin = lambda w: project_in(w, zn, mask_pair)
    (a_f, b_f), pull_in = jax.vjp(fin, w_in)
    _, (ta_f, tb_f) = jax.jvp(fin, (w_in,), (v_in,))
    a_bf, b_bf = (a_f.astype(jnp.bfloat16), b_f.astype(jnp.bfloat16))
    ta_bf, tb_bf = (ta_f.astype(jnp.bfloat16), tb_f.astype(jnp.bfloat16))
    a_ch, b_ch = (
        lax.all_to_all(a_bf, "axial", split_axis=0, concat_axis=1, tiled=True),
        lax.all_to_all(b_bf, "axial", split_axis=0, concat_axis=1, tiled=True),
    )
    ta_ch, tb_ch = (
        lax.all_to_all(ta_bf, "axial", split_axis=0, concat_axis=1, tiled=True),
        lax.all_to_all(tb_bf, "axial", split_axis=0, concat_axis=1, tiled=True),
    )
    x_ch, tx_ch, a_ch, b_ch = slab_products((a_ch, b_ch, ta_ch, tb_ch))
    x_bf, tx_bf = (
        lax.all_to_all(x_ch, "axial", split_axis=1, concat_axis=0, tiled=True),
        lax.all_to_all(tx_ch, "axial", split_axis=1, concat_axis=0, tiled=True),
    )
    fhead = lambda w, xx: head(w, xx, zn)
    out, pull_head = jax.vjp(fhead, w_head, x_bf.astype(jnp.float32))
    _, t_out = jax.jvp(
        fhead, (w_head, x_bf.astype(jnp.float32)), (v_head, tx_bf.astype(jnp.float32))
    )
    total = lax.axis_size("crop") * width * width
    cot = t_out * (1.0 / total)
    g_head, x_bar = pull_head(cot)
    g_head_sum = lax.psum(g_head, ("crop", "axial"))
    xb_ch = lax.all_to_all(
        x_bar.astype(jnp.bfloat16), "axial", split_axis=0, concat_axis=1, tiled=True
    )
    a_bar = jnp.einsum("cij,cjk->cik", xb_ch, b_ch, preferred_element_type=jnp.float32).astype(
        jnp.bfloat16
    )
    b_bar = jnp.einsum("cij,cik->cjk", xb_ch, a_ch, preferred_element_type=jnp.float32).astype(
        jnp.bfloat16
    )
    a_back, b_back = (
        lax.all_to_all(a_bar, "axial", split_axis=1, concat_axis=0, tiled=True),
        lax.all_to_all(b_bar, "axial", split_axis=1, concat_axis=0, tiled=True),
    )
    g_in = pull_in((a_back.astype(jnp.float32), b_back.astype(jnp.float32)))[0]
    g_in_sum = lax.psum(g_in, ("crop", "axial"))
    curvature = jnp.concatenate([g_in_sum, g_head_sum], axis=1)
    new_pair = (pair_rows.astype(jnp.float32) + out).astype(jnp.bfloat16)
    return (new_pair[None], curvature)


def solution(mesh):
    placed = (P("crop", "axial", None, None), P("crop", None), P(), P())
    return jax.shard_map(
        shards,
        mesh=mesh,
        in_specs=placed,
        out_specs=(P("crop", "axial", None, None), P()),
        check_vma=False,
    )
```

profile of v0, /device:TPU:2, one launch (start us, length us, event | category | flops | bytes accessed | tf_op | source)
XLA Modules:
  0.0 779.2 jit_solution(10818521390159609590)
XLA Ops:
  15.0 2.1 fusion.38
  18.0 21.3 %all-to-all-start.4 = ((bf16[128,4,256]{2,1,0:T(4,128)(2,1)}), bf16[128,4,256]{2,1,0:T(4,128)(2,1)S(1)}, u32[]{:S(2)}, u32[]{:S(2)}) async-start(bf16[128,4,256]{2,1,0:T(4,128)(2,1)} %copy.69), calls=%async_computation.4 | async-start | bytes 524288 | tf_op jit(solution)/shard_map/all_to_all | solution.py:73
  40.1 20.7 %all-to-all-done.4 = bf16[128,4,256]{2,1,0:T(4,128)(2,1)S(1)} async-done(((bf16[128,4,256]{2,1,0:T(4,128)(2,1)}), bf16[128,4,256]{2,1,0:T(4,128)(2,1)S(1)}, u32[]{:S(2)}, u32[]{:S(2)}) %all-to-all-start.4) | async-done | bytes 262176 | tf_op jit(solution)/shard_map/all_to_all | solution.py:73
  60.9 7.8 all-to-all-start.1
  69.6 16.7 %all-to-all-done.1 = bf16[128,4,256]{2,1,0:T(4,128)(2,1)S(1)} async-done(((bf16[128,4,256]{2,1,0:T(4,128)(2,1)}), bf16[128,4,256]{2,1,0:T(4,128)(2,1)S(1)}, u32[]{:S(2)}, u32[]{:S(2)}) %all-to-all-start.1) | async-done | bytes 262176 | tf_op jit(solution)/shard_map/all_to_all | solution.py:69
  86.3 9.7 %all-to-all-start = ((bf16[128,4,256]{2,1,0:T(4,128)(2,1)}), bf16[128,4,256]{2,1,0:T(4,128)(2,1)S(1)}, u32[]{:S(2)}, u32[]{:S(2)}) async-start(bf16[128,4,256]{2,1,0:T(4,128)(2,1)} %copy.55), calls=%async_computation | async-start | bytes 524288 | tf_op jit(solution)/shard_map/all_to_all | solution.py:68
  96.8 20.0 %all-to-all-done = bf16[128,4,256]{2,1,0:T(4,128)(2,1)S(1)} async-done(((bf16[128,4,256]{2,1,0:T(4,128)(2,1)}), bf16[128,4,256]{2,1,0:T(4,128)(2,1)S(1)}, u32[]{:S(2)}, u32[]{:S(2)}) %all-to-all-start) | async-done | bytes 262176 | tf_op jit(solution)/shard_map/all_to_all | solution.py:68
  116.8 6.6 all-to-all-start.3
  126.1 18.4 %all-to-all-done.3 = bf16[128,4,256]{2,1,0:T(4,128)(2,1)} async-done(((bf16[128,4,256]{2,1,0:T(4,128)(2,1)}), bf16[128,4,256]{2,1,0:T(4,128)(2,1)}, u32[]{:S(2)}, u32[]{:S(2)}) %all-to-all-start.3) | async-done | bytes 262176 | tf_op jit(solution)/shard_map/all_to_all | solution.py:72
  144.5 6.1 all-to-all-start.2
  158.3 13.6 %all-to-all-done.2 = bf16[2,256,256]{2,0,1:T(2,128)(2,1)S(1)} async-done(((bf16[2,256,256]{2,0,1:T(2,128)(2,1)}), bf16[2,256,256]{2,0,1:T(2,128)(2,1)S(1)}, u32[]{:S(2)}, u32[]{:S(2)}) %all-to-all-start.2) | async-done | bytes 262176 | tf_op jit(solution)/shard_map/all_to_all | solution.py:77
  171.9 7.0 all-to-all-start.5
  184.7 15.3 %all-to-all-done.5 = bf16[2,256,256]{2,0,1:T(2,128)(2,1)} async-done(((bf16[2,256,256]{2,0,1:T(2,128)(2,1)}), bf16[2,256,256]{2,0,1:T(2,128)(2,1)}, u32[]{:S(2)}, u32[]{:S(2)}) %all-to-all-start.5) | async-done | bytes 262176 | tf_op jit(solution)/shard_map/all_to_all | solution.py:78
  202.0 1.9 copy_bitcast_fusion
  204.0 2.2 reshape.106
  206.2 1.9 multiply_reduce_fusion
  214.2 27.7 %all_to_all.126 = bf16[128,4,256]{2,1,0:T(4,128)(2,1)S(1)} all-to-all(bf16[128,4,256]{2,1,0:T(4,128)(2,1)S(1)} %copy.75), channel_id=1, replica_groups=mesh['crop'=8,'axial'=64] {'axial'}, dimensions={0} | all-to-all | bytes 524288 | tf_op jit(solution)/shard_map/all_to_all | solution.py:89
  243.8 6.8 all-to-all-start.8
  252.9 16.5 %all-to-all-done.8 = bf16[2,256,256]{2,0,1:T(2,128)(2,1)} async-done(((bf16[2,256,256]{2,0,1:T(2,128)(2,1)}), bf16[2,256,256]{2,0,1:T(2,128)(2,1)}, u32[]{:S(2)}, u32[]{:S(2)}) %all-to-all-start.8) | async-done | bytes 262176 | tf_op jit(solution)/shard_map/all_to_all | solution.py:99
  269.4 8.6 %all-to-all-start.7 = ((bf16[2,256,256]{2,0,1:T(2,128)(2,1)}), bf16[2,256,256]{2,0,1:T(2,128)(2,1)}, u32[]{:S(2)}, u32[]{:S(2)}) async-start(bf16[2,256,256]{2,0,1:T(2,128)(2,1)} %copy.78), calls=%async_computation.7 | async-start | bytes 524288 | tf_op jit(solution)/shard_map/all_to_all | solution.py:100
  283.5 2.0 copy.84
  285.6 12.7 %all-to-all-done.7 = bf16[2,256,256]{2,0,1:T(2,128)(2,1)} async-done(((bf16[2,256,256]{2,0,1:T(2,128)(2,1)}), bf16[2,256,256]{2,0,1:T(2,128)(2,1)}, u32[]{:S(2)}, u32[]{:S(2)}) %all-to-all-start.7) | async-done | bytes 262176 | tf_op jit(solution)/shard_map/all_to_all | solution.py:100
  300.1 2.1 copy.80
  306.0 464.6 %all-reduce.9.cloned.1.call-done = (f32[128,256]{1,0:T(8,128)}, f32[128,512]{1,0:T(8,128)}) async-done(((f32[128,256]{1,0:T(8,128)}, f32[128,512]{1,0:T(8,128)}), (f32[128,256]{1,0:T(8,128)}, f32[128,512]{1,0:T(8,128)})) %all-reduce.9.cloned.1.call-update) | async-done | bytes 393232 | tf_op jit(solution)/shard_map/psum | solution.py:88
  (93 shorter events, 52.4 us)
Async XLA Ops:
  7.2 5.8 copy-start
  11.4 3.4 copy-start.14
  18.0 42.9 %all-to-all-start.4 = ((bf16[128,4,256]{2,1,0:T(4,128)(2,1)}), bf16[128,4,256]{2,1,0:T(4,128)(2,1)S(1)}, u32[]{:S(2)}, u32[]{:S(2)}) async-start(bf16[128,4,256]{2,1,0:T(4,128)(2,1)} %copy.69), calls=%async_computation.4 | async-start | bytes 524288 | tf_op jit(solution)/shard_map/all_to_all | solution.py:73
  60.9 25.4 %all-to-all-start.1 = ((bf16[128,4,256]{2,1,0:T(4,128)(2,1)}), bf16[128,4,256]{2,1,0:T(4,128)(2,1)S(1)}, u32[]{:S(2)}, u32[]{:S(2)}) async-start(bf16[128,4,256]{2,1,0:T(4,128)(2,1)} %copy.57), calls=%async_computation.1 | async-start | bytes 524288 | tf_op jit(solution)/shard_map/all_to_all | solution.py:69
  86.3 30.6 %all-to-all-start = ((bf16[128,4,256]{2,1,0:T(4,128)(2,1)}), bf16[128,4,256]{2,1,0:T(4,128)(2,1)S(1)}, u32[]{:S(2)}, u32[]{:S(2)}) async-start(bf16[128,4,256]{2,1,0:T(4,128)(2,1)} %copy.55), calls=%async_computation | async-start | bytes 524288 | tf_op jit(solution)/shard_map/all_to_all | solution.py:68
  116.8 6.6 copy-start.13
  116.8 27.6 %all-to-all-start.3 = ((bf16[128,4,256]{2,1,0:T(4,128)(2,1)}), bf16[128,4,256]{2,1,0:T(4,128)(2,1)}, u32[]{:S(2)}, u32[]{:S(2)}) async-start(bf16[128,4,256]{2,1,0:T(4,128)(2,1)} %copy.65), calls=%async_computation.3 | async-start | bytes 524288 | tf_op jit(solution)/shard_map/all_to_all | solution.py:72
  123.6 32.2 %copy-start.8 = (bf16[2,256,256]{2,1,0:T(8,128)(2,1)}, bf16[2,256,256]{2,1,0:T(8,128)(2,1)S(1)}, u32[]{:S(2)}) copy-start(bf16[2,256,256]{2,1,0:T(8,128)(2,1)S(1)} %all_to_all.100) | copy-start | bytes 786436
  124.8 32.2 %copy-start.6 = (bf16[2,256,256]{2,1,0:T(8,128)(2,1)}, bf16[2,256,256]{2,1,0:T(8,128)(2,1)S(1)}, u32[]{:S(2)}) copy-start(bf16[2,256,256]{2,1,0:T(8,128)(2,1)S(1)} %all_to_all.96) | copy-start | bytes 786436
  144.5 27.4 %all-to-all-start.2 = ((bf16[2,256,256]{2,0,1:T(2,128)(2,1)}), bf16[2,256,256]{2,0,1:T(2,128)(2,1)S(1)}, u32[]{:S(2)}, u32[]{:S(2)}) async-start(bf16[2,256,256]{2,0,1:T(2,128)(2,1)} %copy.59), calls=%async_computation.2 | async-start | bytes 524288 | tf_op jit(solution)/shard_map/all_to_all | solution.py:77
  171.9 8.3 %copy-start.10 = (bf16[2,256,256]{2,0,1:T(2,128)(2,1)}, bf16[2,256,256]{2,0,1:T(2,128)(2,1)S(1)}, u32[]{:S(2)}) copy-start(bf16[2,256,256]{2,0,1:T(2,128)(2,1)S(1)} %all-to-all-done.2) | copy-start | bytes 786436
  171.9 28.1 %all-to-all-start.5 = ((bf16[2,256,256]{2,0,1:T(2,128)(2,1)}), bf16[2,256,256]{2,0,1:T(2,128)(2,1)}, u32[]{:S(2)}, u32[]{:S(2)}) async-start(bf16[2,256,256]{2,0,1:T(2,128)(2,1)} %copy.71), calls=%async_computation.5 | async-start | bytes 524288 | tf_op jit(solution)/shard_map/all_to_all | solution.py:78
  183.7 0.8 copy-start.4
  201.1 0.8 copy-start.5
  206.2 3.0 copy-start.12
  208.2 2.2 copy-start.7
  209.2 3.4 copy-start.1
  212.6 1.4 copy-start.3
  213.7 28.4 %copy-start.9 = (bf16[2,256,256]{2,1,0:T(8,128)(2,1)S(1)}, bf16[2,256,256]{2,1,0:T(8,128)(2,1)}, u32[]{:S(2)}) copy-start(bf16[2,256,256]{2,1,0:T(8,128)(2,1)} %copy-done.8) | copy-start | bytes 786436
  242.1 0.7 copy-start.11
  242.8 36.6 %copy-start.2 = (f32[4,256,128]{2,1,0:T(8,128)S(1)}, f32[4,256,128]{2,1,0:T(8,128)}, u32[]{:S(2)}) copy-start(f32[4,256,128]{2,1,0:T(8,128)} %copy-done.1) | copy-start | bytes 1572868
  243.8 25.6 %all-to-all-start.8 = ((bf16[2,256,256]{2,0,1:T(2,128)(2,1)}), bf16[2,256,256]{2,0,1:T(2,128)(2,1)}, u32[]{:S(2)}, u32[]{:S(2)}) async-start(bf16[2,256,256]{2,0,1:T(2,128)(2,1)} %copy.82), calls=%async_computation.8 | async-start | bytes 524288 | tf_op jit(solution)/shard_map/all_to_all | solution.py:99
  269.4 28.8 %all-to-all-start.7 = ((bf16[2,256,256]{2,0,1:T(2,128)(2,1)}), bf16[2,256,256]{2,0,1:T(2,128)(2,1)}, u32[]{:S(2)}, u32[]{:S(2)}) async-start(bf16[2,256,256]{2,0,1:T(2,128)(2,1)} %copy.78), calls=%async_computation.7 | async-start | bytes 524288 | tf_op jit(solution)/shard_map/all_to_all | solution.py:100
  278.0 492.6 %all-reduce.9.cloned.1.call-start = ((), (), s32[]{:S(2)}) async-start(), calls=%async_computation.9 | async-start | bytes 786432 | tf_op jit(solution)/shard_map/psum | solution.py:88
Sparse Core Ops, SparseCore 0:
  305.3 465.2 all-reduce.8
where the time goes:
time: 781 us; the launch traced here: 779 us
  waiting for transfers between devices  598 us (77%)
  starting transfers between devices  73.9 us (9%)
  local copies, waits for them, and re-layouts  28.1 us (4%)
  blocking collectives  27.7 us (4%)
  other arithmetic  18.9 us (2%)
  matrix products  17.7 us (2%)
  between operations  14.5 us (2%)
    psum x1, waiting for transfers between devices, shards(): g_head_sum = lax.psum(g_head, ('crop', 'axial'))  465 us
    all_to_all x1, blocking collectives, shards(): lax.all_to_all(x_bar.astype(jnp.bfloat16), 'axial', split_axis=0, concat_...  27.7 us
    all_to_all x1, starting transfers between devices, shards(): lax.all_to_all(tb_bf, 'axial', split_axis=0, concat_axis=1, tiled=True)  21.3 us
    all_to_all x1, waiting for transfers between devices, shards(): lax.all_to_all(tb_bf, 'axial', split_axis=0, concat_axis=1, tiled=True)  20.7 us
    all_to_all x1, waiting for transfers between devices, shards(): lax.all_to_all(a_bf, 'axial', split_axis=0, concat_axis=1, tiled=True)  20 us
    all_to_all x1, waiting for transfers between devices, shards(): lax.all_to_all(ta_bf, 'axial', split_axis=0, concat_axis=1, tiled=True)  18.4 us
    all_to_all x1, waiting for transfers between devices, shards(): lax.all_to_all(b_bf, 'axial', split_axis=0, concat_axis=1, tiled=True)  16.7 us
    all_to_all x1, waiting for transfers between devices, shards(): lax.all_to_all(a_bar, 'axial', split_axis=1, concat_axis=0, tiled=True)  16.5 us
  transfers between devices with their start and end apart: 9, of which 9 were waited for; matrix products, arithmetic and copies ran while one was open for 3% of the time, Pallas kernels for 0%

commit v1 on v0

--- a/solution.py
+++ b/solution.py
@@ -85,7 +85,7 @@
     total = lax.axis_size("crop") * width * width
     cot = t_out * (1.0 / total)
     g_head, x_bar = pull_head(cot)
-    g_head_sum = lax.psum(g_head, ("crop", "axial"))
+    g_head_sum = lax.psum(lax.psum(g_head, "axial"), "crop")
     xb_ch = lax.all_to_all(
         x_bar.astype(jnp.bfloat16), "axial", split_axis=0, concat_axis=1, tiled=True
     )

time: 781 us -> 1630 us (2.09)
  the two profiles are of different devices: /device:TPU:2 before, /device:TPU:4 now
where the time goes in v1:
time: 1630 us
  waiting for transfers between devices  1440 us (88%)
  starting transfers between devices  83.8 us (5%)
  local copies, waits for them, and re-layouts  28.1 us (2%)
  blocking collectives  28 us (2%)
  other arithmetic  18.9 us (1%)
  matrix products  17.6 us (1%)
    psum x2, waiting for transfers between devices, shards(): g_head_sum = lax.psum(lax.psum(g_head, 'axial'), 'crop')  856 us
    psum x1, waiting for transfers between devices, shards(): g_in_sum = lax.psum(g_in, ('crop', 'axial'))  471 us
  transfers between devices with their start and end apart: 11, of which 10 were waited for; matrix products, arithmetic and copies ran while one was open for 2% of the time, Pallas kernels for 0%

profile of v1, /device:TPU:4, one launch (start us, length us, event | category | flops | bytes accessed | tf_op | source)
XLA Modules:
  0.0 1628.2 jit_solution(13380235310690939671)
XLA Ops:
  14.9 2.1 fusion.38
  18.0 21.3 %all-to-all-start.4 = ((bf16[128,4,256]{2,1,0:T(4,128)(2,1)}), bf16[128,4,256]{2,1,0:T(4,128)(2,1)S(1)}, u32[]{:S(2)}, u32[]{:S(2)}) async-start(bf16[128,4,256]{2,1,0:T(4,128)(2,1)} %copy.69), calls=%async_computation.4 | async-start | bytes 524288 | tf_op jit(solution)/shard_map/all_to_all | solution.py:73
  40.2 19.4 %all-to-all-done.4 = bf16[128,4,256]{2,1,0:T(4,128)(2,1)S(1)} async-done(((bf16[128,4,256]{2,1,0:T(4,128)(2,1)}), bf16[128,4,256]{2,1,0:T(4,128)(2,1)S(1)}, u32[]{:S(2)}, u32[]{:S(2)}) %all-to-all-start.4) | async-done | bytes 262176 | tf_op jit(solution)/shard_map/all_to_all | solution.py:73
  59.6 9.2 all-to-all-start.1
  69.6 15.2 all-to-all-done.1
  84.8 11.2 all-to-all-start
  96.9 18.5 %all-to-all-done = bf16[128,4,256]{2,1,0:T(4,128)(2,1)S(1)} async-done(((bf16[128,4,256]{2,1,0:T(4,128)(2,1)}), bf16[128,4,256]{2,1,0:T(4,128)(2,1)S(1)}, u32[]{:S(2)}, u32[]{:S(2)}) %all-to-all-start) | async-done | bytes 262176 | tf_op jit(solution)/shard_map/all_to_all | solution.py:68
  115.4 8.1 all-to-all-start.3
  126.1 16.9 %all-to-all-done.3 = bf16[128,4,256]{2,1,0:T(4,128)(2,1)} async-done(((bf16[128,4,256]{2,1,0:T(4,128)(2,1)}), bf16[128,4,256]{2,1,0:T(4,128)(2,1)}, u32[]{:S(2)}, u32[]{:S(2)}) %all-to-all-start.3) | async-done | bytes 262176 | tf_op jit(solution)/shard_map/all_to_all | solution.py:72
  143.1 7.5 all-to-all-start.2
  158.4 12.2 all-to-all-done.2
  170.6 8.5 all-to-all-start.5
  184.8 13.8 all-to-all-done.5
  200.7 1.9 copy_bitcast_fusion
  202.6 2.2 reshape.106
  212.8 28.0 %all_to_all.126 = bf16[128,4,256]{2,1,0:T(4,128)(2,1)S(1)} all-to-all(bf16[128,4,256]{2,1,0:T(4,128)(2,1)S(1)} %copy.75), channel_id=1, replica_groups=mesh['crop'=8,'axial'=64] {'axial'}, dimensions={0} | all-to-all | bytes 524288 | tf_op jit(solution)/shard_map/all_to_all | solution.py:89
  242.7 7.9 all-to-all-start.8
  252.9 15.1 all-to-all-done.8
  268.0 9.9 all-to-all-start.7
  281.7 771.4 %all-reduce.12.cloned.1.call-done = f32[128,256]{1,0:T(8,128)} async-done(((f32[128,256]{1,0:T(8,128)}), f32[128,256]{1,0:T(8,128)}) %all-reduce.12.cloned.1.call-update) | async-done | bytes 131088 | tf_op jit(solution)/shard_map/psum | solution.py:88
  1055.0 2.0 copy.84
  1058.9 2.1 copy.80
  1064.8 84.4 %all-reduce.14.cloned.1.call-done = f32[128,256]{1,0:T(8,128)} async-done(((f32[128,256]{1,0:T(8,128)}), f32[128,256]{1,0:T(8,128)}) %all-reduce.14.cloned.1.call-update) | async-done | bytes 131088 | tf_op jit(solution)/shard_map/psum | solution.py:88
  1149.2 470.7 %all-reduce.10.cloned.1.call-done = f32[128,512]{1,0:T(8,128)} async-done(((f32[128,512]{1,0:T(8,128)}), f32[128,512]{1,0:T(8,128)}) %all-reduce.10.cloned.1.call-update) | async-done | bytes 262160 | tf_op jit(solution)/shard_map/psum | solution.py:103
  (99 shorter events, 54.4 us)
Async XLA Ops:
  7.2 5.8 copy-start
  11.4 3.4 copy-start.14
  18.0 41.6 %all-to-all-start.4 = ((bf16[128,4,256]{2,1,0:T(4,128)(2,1)}), bf16[128,4,256]{2,1,0:T(4,128)(2,1)S(1)}, u32[]{:S(2)}, u32[]{:S(2)}) async-start(bf16[128,4,256]{2,1,0:T(4,128)(2,1)} %copy.69), calls=%async_computation.4 | async-start | bytes 524288 | tf_op jit(solution)/shard_map/all_to_all | solution.py:73
  59.6 25.2 %all-to-all-start.1 = ((bf16[128,4,256]{2,1,0:T(4,128)(2,1)}), bf16[128,4,256]{2,1,0:T(4,128)(2,1)S(1)}, u32[]{:S(2)}, u32[]{:S(2)}) async-start(bf16[128,4,256]{2,1,0:T(4,128)(2,1)} %copy.57), calls=%async_computation.1 | async-start | bytes 524288 | tf_op jit(solution)/shard_map/all_to_all | solution.py:69
  84.8 30.6 %all-to-all-start = ((bf16[128,4,256]{2,1,0:T(4,128)(2,1)}), bf16[128,4,256]{2,1,0:T(4,128)(2,1)S(1)}, u32[]{:S(2)}, u32[]{:S(2)}) async-start(bf16[128,4,256]{2,1,0:T(4,128)(2,1)} %copy.55), calls=%async_computation | async-start | bytes 524288 | tf_op jit(solution)/shard_map/all_to_all | solution.py:68
  115.4 8.1 copy-start.13
  115.4 27.6 %all-to-all-start.3 = ((bf16[128,4,256]{2,1,0:T(4,128)(2,1)}), bf16[128,4,256]{2,1,0:T(4,128)(2,1)}, u32[]{:S(2)}, u32[]{:S(2)}) async-start(bf16[128,4,256]{2,1,0:T(4,128)(2,1)} %copy.65), calls=%async_computation.3 | async-start | bytes 524288 | tf_op jit(solution)/shard_map/all_to_all | solution.py:72
  123.7 32.2 %copy-start.8 = (bf16[2,256,256]{2,1,0:T(8,128)(2,1)}, bf16[2,256,256]{2,1,0:T(8,128)(2,1)S(1)}, u32[]{:S(2)}) copy-start(bf16[2,256,256]{2,1,0:T(8,128)(2,1)S(1)} %all_to_all.100) | copy-start | bytes 786436
  124.9 32.2 %copy-start.6 = (bf16[2,256,256]{2,1,0:T(8,128)(2,1)}, bf16[2,256,256]{2,1,0:T(8,128)(2,1)S(1)}, u32[]{:S(2)}) copy-start(bf16[2,256,256]{2,1,0:T(8,128)(2,1)S(1)} %all_to_all.96) | copy-start | bytes 786436
  143.1 27.5 %all-to-all-start.2 = ((bf16[2,256,256]{2,0,1:T(2,128)(2,1)}), bf16[2,256,256]{2,0,1:T(2,128)(2,1)S(1)}, u32[]{:S(2)}, u32[]{:S(2)}) async-start(bf16[2,256,256]{2,0,1:T(2,128)(2,1)} %copy.59), calls=%async_computation.2 | async-start | bytes 524288 | tf_op jit(solution)/shard_map/all_to_all | solution.py:77
  170.6 9.8 copy-start.10
  170.6 28.0 %all-to-all-start.5 = ((bf16[2,256,256]{2,0,1:T(2,128)(2,1)}), bf16[2,256,256]{2,0,1:T(2,128)(2,1)}, u32[]{:S(2)}, u32[]{:S(2)}) async-start(bf16[2,256,256]{2,0,1:T(2,128)(2,1)} %copy.71), calls=%async_computation.5 | async-start | bytes 524288 | tf_op jit(solution)/shard_map/all_to_all | solution.py:78
  199.7 0.8 copy-start.5
  204.8 3.0 copy-start.12
  206.8 2.2 copy-start.7
  207.8 3.4 copy-start.1
  211.2 1.4 copy-start.3
  212.3 28.7 %copy-start.9 = (bf16[2,256,256]{2,1,0:T(8,128)(2,1)S(1)}, bf16[2,256,256]{2,1,0:T(8,128)(2,1)}, u32[]{:S(2)}) copy-start(bf16[2,256,256]{2,1,0:T(8,128)(2,1)} %copy-done.8) | copy-start | bytes 786436
  241.7 37.7 %copy-start.2 = (f32[4,256,128]{2,1,0:T(8,128)S(1)}, f32[4,256,128]{2,1,0:T(8,128)}, u32[]{:S(2)}) copy-start(f32[4,256,128]{2,1,0:T(8,128)} %copy-done.1) | copy-start | bytes 1572868
  242.7 25.3 %all-to-all-start.8 = ((bf16[2,256,256]{2,0,1:T(2,128)(2,1)}), bf16[2,256,256]{2,0,1:T(2,128)(2,1)}, u32[]{:S(2)}, u32[]{:S(2)}) async-start(bf16[2,256,256]{2,0,1:T(2,128)(2,1)} %copy.82), calls=%async_computation.8 | async-start | bytes 524288 | tf_op jit(solution)/shard_map/all_to_all | solution.py:99
  268.0 789.0 %all-to-all-start.7 = ((bf16[2,256,256]{2,0,1:T(2,128)(2,1)}), bf16[2,256,256]{2,0,1:T(2,128)(2,1)}, u32[]{:S(2)}, u32[]{:S(2)}) async-start(bf16[2,256,256]{2,0,1:T(2,128)(2,1)} %copy.78), calls=%async_computation.7 | async-start | bytes 524288 | tf_op jit(solution)/shard_map/all_to_all | solution.py:100
  278.0 775.1 %all-reduce.12.cloned.1.call-start = ((), (), s32[]{:S(2)}) async-start(), calls=%async_computation.10 | async-start | bytes 262144 | tf_op jit(solution)/shard_map/psum | solution.py:88
  281.7 867.6 %all-reduce.14.cloned.1.call-start = ((), (), s32[]{:S(2)}) async-start(), calls=%async_computation.11 | async-start | bytes 262144 | tf_op jit(solution)/shard_map/psum | solution.py:88
  1053.1 566.8 %all-reduce.10.cloned.1.call-start = ((), (), s32[]{:S(2)}) async-start(), calls=%async_computation.9 | async-start | bytes 524288 | tf_op jit(solution)/shard_map/psum | solution.py:103
  (2 other events, 1.5 us)
Sparse Core Ops, SparseCore 0:
  282.3 770.7 all-reduce.11
  1056.0 93.2 all-reduce.13
  1155.3 464.6 all-reduce.9
